TPU v7x, 128 devices: a whole 4x4x4 slice. The times are simulated.
128 devices in a mesh: gx: 4 (over z_hi, core), gy: 4 (over y), gz: 8 (over z_lo, x).
Axes of the slice: x: 4, y: 4, z: 4 (z_hi: 2, z_lo: 2; z = z_hi * 2 + z_lo), core: 2. Of those that a mesh axis runs over, the one named last changes fastest.
Arguments:
- grads: bfloat16 [8, 2048, 3584], P('gz', ('gx', 'gy')), may hold values from -300 to 300
- momentum: float32 [2048, 3584], P(('gx', 'gy')), may hold values from -0.8 to 0.8
- variance: float32 [2048, 3584], P(('gx', 'gy'), 'gz'), may hold values from 0.25 to 4
- master: float32 [2048, 3584], P(('gx', 'gy', 'gz')), may hold values from -6 to 6
Outputs:
- weights: bfloat16 [2048, 3584], replicated
- new_master: float32 [2048, 3584], P(('gx', 'gy', 'gz'))
- new_momentum: float32 [2048, 3584], P(('gx', 'gy', 'gz'))
- worker_error: float32 [8, 2048, 3584], P('gz', ('gx', 'gy'))
All inputs are finite; a program needn't handle non-finite values.
Results may differ from a plain program's by a relative error of at most 0.007.
Values may be sent and summed in bfloat16 or wider, within the bound.
A program may use at most 128 MiB of HBM per device.

v0:
```python
import jax
import jax.numpy as jnp
from jax import lax
from jax.sharding import PartitionSpec as P

beta_one = 0.9
learning_rate = 0.25
epsilon = 1e-08


def from_everyone(x, axis):
    copies = jnp.broadcast_to(x, (lax.axis_size(axis), *x.shape))
    return lax.all_to_all(copies, axis, split_axis=0, concat_axis=0, tiled=True)


def joined_along(blocks, dim):
    blocks = jnp.moveaxis(blocks, 0, dim)
    shape = blocks.shape
    return blocks.reshape(*shape[:dim], shape[dim] * shape[dim + 1], *shape[dim + 2 :])


def collect(x, axis, dim):
    blocks = from_everyone(x, axis)
    return joined_along(blocks, dim)


def shards(grads, momentum, variance, master):
    owned_variance = lax.all_to_all(
        variance.astype(jnp.bfloat16), "gz", split_axis=0, concat_axis=1, tiled=True
    ).astype(variance.dtype)
    corrected = beta_one * momentum + (1.0 - beta_one) * grads[0].astype(jnp.float32)
    level = jnp.mean(jnp.abs(corrected), axis=-1, keepdims=True).astype(jnp.bfloat16)
    signs = jnp.where(corrected >= 0.0, 1.0, -1.0).astype(jnp.float32)
    compressed = (level.astype(jnp.float32) * signs).astype(jnp.bfloat16)
    worker_error = (corrected - compressed.astype(jnp.float32))[None]
    received = lax.all_to_all(compressed[:, None, :], "gz", split_axis=0, concat_axis=1, tiled=True)
    new_momentum = jnp.sum(received.astype(jnp.float32), axis=1) / received.shape[1]
    new_master = master - learning_rate * new_momentum / (jnp.sqrt(owned_variance) + epsilon)
    shard = new_master.astype(jnp.bfloat16)
    gathered = collect(shard, "gz", 0)
    weights = lax.all_gather(gathered, ("gx", "gy"), axis=0, tiled=True)
    return (weights, new_master, new_momentum, worker_error)


def solution(mesh):
    return jax.shard_map(
        shards,
        mesh=mesh,
        in_specs=(
            P("gz", ("gx", "gy"), None),
            P(("gx", "gy"), None),
            P(("gx", "gy"), "gz"),
            P(("gx", "gy", "gz"), None),
        ),
        out_specs=(
            P(),
            P(("gx", "gy", "gz"), None),
            P(("gx", "gy", "gz"), None),
            P("gz", ("gx", "gy"), None),
        ),
        check_vma=False,
    )
```

profile of v0, /device:TPU:1, one launch (start us, length us, event | category | flops | bytes accessed | tf_op | source)
XLA Modules:
  0.0 189.1 jit_solution(6112298998503527955)
XLA Ops:
  7.2 0.0 copy-start
  7.2 0.0 copy-start.1
  7.2 1.8 copy.15
  9.0 6.2 %all-to-all-start.1 = ((bf16[8,16,448]{2,1,0:T(8,128)(2,1)}), bf16[8,16,448]{2,1,0:T(8,128)(2,1)S(1)}, u32[]{:S(2)}, u32[]{:S(2)}) async-start(bf16[8,16,448]{2,1,0:T(8,128)(2,1)} %bitcast.2), calls=%async_computation.1 | async-start | bytes 262144 | tf_op jit(solution)/shard_map/all_to_all | solution.py:28
  15.2 2.2 %abs_reduce_fusion = f32[128]{0:T(128)S(1)} fusion(bf16[1,128,3584]{2,1,0:T(8,128)(2,1)} %param.4, f32[128,3584]{1,0:T(8,128)} %param.5), kind=kLoop, calls=%fused_computation.3 | loop fusion | flops 2752384 | bytes 2753024 | tf_op jit(solution)/shard_map/reduce_sum | solution.py:32
  17.5 0.0 copy-done
  17.5 0.0 copy-done.1
  17.5 2.1 %subtract_bitcast_fusion = (f32[1,128,3584]{2,1,0:T(8,128)}, bf16[128,1,3584]{2,0,1:T(8,128)(2,1)}) fusion(f32[128]{0:T(128)S(1)} %convert_convert_fusion, bf16[1,128,3584]{2,1,0:T(8,128)(2,1)S(1)} %copy-done.1, f32[128,3584]{1,0:T(8,128)S(1)} %copy-done), kind=kLoop, calls=%fused_computation.1 | loop fusion | flops 4587520 | bytes 5505536 | tf_op jit(solution)/shard_map/broadcast_in_dim | solution.py:35
  19.5 0.5 broadcast.14
  20.0 2.5 %reduce.3 = bf16[128,3584]{1,0:T(8,128)(2,1)S(1)} reduce(bf16[128,1,3584]{2,0,1:T(8,128)(2,1)} %get-tuple-element.7, bf16[]{:T(256)} %broadcast.14), dimensions={1}, to_apply=%copy.14.reduce_sub_computation | reduce | bytes 1835010 | tf_op jit(solution)/shard_map/broadcast_in_dim | solution.py:36
  22.5 1.6 reshape.35
  24.1 0.0 all-to-all-done.1
  24.1 5.1 %all-to-all-start = ((bf16[8,2,28672]{2,1,0:T(2,128)(2,1)}), bf16[8,2,28672]{2,1,0:T(2,128)(2,1)S(1)}, u32[]{:S(2)}, u32[]{:S(2)}) async-start(bf16[8,2,28672]{2,1,0:T(2,128)(2,1)} %reshape.35), calls=%async_computation | async-start | bytes 1835008 | tf_op jit(solution)/shard_map/all_to_all | solution.py:36
  29.3 0.0 all-gather.2.cloned.1.call-start
  29.3 0.1 add_bitcast_fusion
  29.4 0.2 copy.16
  29.6 0.1 add.19
  29.7 14.0 %all-to-all-done = bf16[8,2,28672]{2,1,0:T(2,128)(2,1)S(1)} async-done(((bf16[8,2,28672]{2,1,0:T(2,128)(2,1)}), bf16[8,2,28672]{2,1,0:T(2,128)(2,1)S(1)}, u32[]{:S(2)}, u32[]{:S(2)}) %all-to-all-start) | async-done | bytes 917536 | tf_op jit(solution)/shard_map/all_to_all | solution.py:36
  43.7 3.3 %reshape.36 = bf16[128,1,3584]{2,1,0:T(2,128)(2,1)} reshape(bf16[8,2,28672]{2,1,0:T(2,128)(2,1)S(1)} %all-to-all-done) | data formatting | bytes 1835008
  47.0 1.6 copy.17
  48.6 0.0 copy-start.2
  48.7 0.1 reduce_sum.19
  48.8 0.8 copy-done.2
  49.6 0.8 fusion.1
  50.4 0.1 broadcast_in_dim.21
  50.5 17.1 %all_to_all.27 = bf16[8,16,3584]{2,1,0:T(8,128)(2,1)} all-to-all(bf16[8,16,3584]{2,1,0:T(8,128)(2,1)S(1)} %broadcast_in_dim.21), channel_id=1, replica_groups=mesh['gx'=4,'gy'=4,'gz'=8] {'gz'}, dimensions={0} | all-to-all | bytes 1835008 | tf_op jit(solution)/shard_map/all_to_all | solution.py:13
  67.5 0.0 all-gather.2.cloned.1.call-update
  67.6 101.6 %all-gather.2.cloned.1.call-done = bf16[2048,3584]{1,0:T(8,128)(2,1)} async-done(((bf16[128,3584]{1,0:T(8,128)(2,1)}), bf16[2048,3584]{1,0:T(8,128)(2,1)}) %all-gather.2.cloned.1.call-update) | async-done | bytes 14680080 | tf_op jit(solution)/shard_map/all_gather | solution.py:41
  169.2 13.1 %copy.20 = bf16[2048,3584]{1,0:T(8,128)(2,1)} copy(bf16[2048,3584]{1,0:T(8,128)(2,1)} %all-gather.2.cloned.1.call-done) | data formatting | bytes 29360128
  (1 shorter events, 0.0 us)
Async XLA Ops:
  7.2 10.3 %copy-start = (f32[128,3584]{1,0:T(8,128)S(1)}, f32[128,3584]{1,0:T(8,128)}, u32[]{:S(2)}) copy-start(f32[128,3584]{1,0:T(8,128)} %param.5) | copy-start | bytes 5505028
  7.2 10.3 %copy-start.1 = (bf16[1,128,3584]{2,1,0:T(8,128)(2,1)S(1)}, bf16[1,128,3584]{2,1,0:T(8,128)(2,1)}, u32[]{:S(2)}) copy-start(bf16[1,128,3584]{2,1,0:T(8,128)(2,1)} %param.4) | copy-start | bytes 2752516
  9.0 15.1 %all-to-all-start.1 = ((bf16[8,16,448]{2,1,0:T(8,128)(2,1)}), bf16[8,16,448]{2,1,0:T(8,128)(2,1)S(1)}, u32[]{:S(2)}, u32[]{:S(2)}) async-start(bf16[8,16,448]{2,1,0:T(8,128)(2,1)} %bitcast.2), calls=%async_computation.1 | async-start | bytes 262144 | tf_op jit(solution)/shard_map/all_to_all | solution.py:28
  24.1 19.6 %all-to-all-start = ((bf16[8,2,28672]{2,1,0:T(2,128)(2,1)}), bf16[8,2,28672]{2,1,0:T(2,128)(2,1)S(1)}, u32[]{:S(2)}, u32[]{:S(2)}) async-start(bf16[8,2,28672]{2,1,0:T(2,128)(2,1)} %reshape.35), calls=%async_computation | async-start | bytes 1835008 | tf_op jit(solution)/shard_map/all_to_all | solution.py:36
  29.3 139.9 %all-gather.2.cloned.1.call-start = ((), (), s32[]{:S(2)}) async-start(), calls=%async_computation.3 | async-start | bytes 15597568 | tf_op jit(solution)/shard_map/all_gather | solution.py:41
  48.6 0.9 copy-start.2
Sparse Core Ops, SparseCore 0:
  67.7 101.4 all-gather.1
where the time goes:
time: 190 us; the launch traced here: 189 us
  waiting for transfers between devices  116 us (61%)
  local copies, waits for them, and re-layouts  23.2 us (12%)
  blocking collectives  17.1 us (9%)
  between operations  14.1 us (7%)
  starting transfers between devices  11.4 us (6%)
  other arithmetic  7.75 us (4%)
    all_gather x1, waiting for transfers between devices, shards(): weights = lax.all_gather(gathered, ('gx', 'gy'), axis=0, tiled=True)  102 us
    unnamed x11, local copies, waits for them, and re-layouts  22.3 us
    all_to_all x1, blocking collectives, from_everyone(): return lax.all_to_all(copies, axis, split_axis=0, concat_axis=0, tiled=True)  17.1 us
    all_to_all x1, waiting for transfers between devices, shards(): lax.all_to_all(compressed[:, None, :], 'gz', split_axis=0, concat_axis=1,...  14 us
    all_to_all x1, starting transfers between devices, shards(): lax.all_to_all(variance.astype(jnp.bfloat16), 'gz', split_axis=0, concat_...  6.19 us
    all_to_all x1, starting transfers between devices, shards(): lax.all_to_all(compressed[:, None, :], 'gz', split_axis=0, concat_axis=1,...  5.14 us
  transfers between devices with their start and end apart: 3, of which 2 were waited for; matrix products, arithmetic and copies ran while one was open for 5% of the time, Pallas kernels for 0%

commit v1 on v0

v1 whole, which is shorter than its diff:
```python
import jax
import jax.numpy as jnp
from jax import lax
from jax.experimental import pallas as pl
from jax.experimental.pallas import tpu as pltpu
from jax.sharding import PartitionSpec as P

beta_one = 0.9
learning_rate = 0.25
epsilon = 1e-08

MESH = pl.DeviceIdType.MESH
WORKERS = 8
ROWS = 16
WIDTH = 3584
PIECE = WIDTH // WORKERS
BLOCKS = 128

COLUMNS = ((0, 1280), (1280, 1152), (2432, 1152))
DIMS = (("x", "y", "z"), ("y", "z", "x"), ("z", "x", "y"))


def block_index(p):
    return (((p["z"] // 2) * 2 + p["c"]) * 4 + p["y"]) * 8 + (p["z"] % 2) * 4 + p["x"]


def device(p):
    return ((p["z"] // 2) * 2 + p["c"], p["y"], (p["z"] % 2) * 4 + p["x"])


def moved(p, dim, by):
    q = dict(p)
    q[dim] = lax.rem(p[dim] + by + 4, 4)
    return q


def line(w, p, color, half=None):
    start, size = COLUMNS[color]
    cols = pl.ds(start, size)
    first = DIMS[color][0]
    part = slice(None) if half is None else pl.ds(half * 2, 2)
    zh, zl = p["z"] // 2, p["z"] % 2
    if first == "x":
        return w.at[zh, p["c"], p["y"], zl, part, :, cols]
    if first == "y":
        return w.at[zh, p["c"], part, zl, p["x"], :, cols]
    if half is None:
        return w.at[:, p["c"], p["y"], :, p["x"], :, cols]
    return w.at[half, p["c"], p["y"], :, p["x"], :, cols]


def unit(w, p, color):
    start, size = COLUMNS[color]
    return w.at[p["z"] // 2, p["c"], p["y"], p["z"] % 2, p["x"], :, pl.ds(start, size)]


def step_kernel(
    g_ref, m_ref, v_ref, master_ref,
    w, new_master_ref, new_momentum_ref, error_ref,
    sent, received, var_sent, var_received,
    send_sem, exchange_sem, var_sem, gather_sem, relay_sem, relay_send_sem, var_send_sem, exchange_send_sem,
):
    gx, gy, gz = lax.axis_index("gx"), lax.axis_index("gy"), lax.axis_index("gz")
    me = {"x": lax.rem(gz, 4), "y": gy, "z": (gx // 2) * 2 + gz // 4, "c": lax.rem(gx, 2)}
    partner = dict(me, c=1 - me["c"])

    barrier = pltpu.get_barrier_semaphore()
    greeted = [(gx, gy, lax.rem(gz + k, WORKERS)) for k in range(1, WORKERS)]
    greeted += [device(moved(me, "y", k)) for k in (1, 2, 3)]
    greeted += [device(moved(me, "z", k)) for k in (1, 2, 3)]
    greeted += [device(partner)]

    for d in greeted:
        pl.semaphore_signal(barrier, inc=1, device_id=d, device_id_type=MESH)

    var = v_ref[...].T.astype(jnp.bfloat16)
    for k in range(WORKERS):
        var_sent[k] = var[k * ROWS:(k + 1) * ROWS, :]

    def compress(owner):
        rows = pl.ds(pl.multiple_of(owner * ROWS, ROWS), ROWS)
        corrected = beta_one * m_ref[rows, :] + (1.0 - beta_one) * g_ref[0, rows, :].astype(jnp.float32)
        level = jnp.mean(jnp.abs(corrected), axis=-1, keepdims=True).astype(jnp.bfloat16).astype(jnp.float32)
        compressed = jnp.where(corrected >= 0.0, level, -level)
        sent[owner] = compressed.astype(jnp.bfloat16)
        error_ref[rows, :] = corrected - compressed

    def exchange(k):
        owner = lax.rem(gz + k, WORKERS)
        return pltpu.make_async_remote_copy(
            src_ref=sent.at[owner], dst_ref=received.at[gz],
            send_sem=exchange_send_sem.at[k], recv_sem=exchange_sem.at[WORKERS - k],
            device_id=(gx, gy, owner), device_id_type=MESH)

    def var_exchange(k):
        owner = lax.rem(gz + k, WORKERS)
        return pltpu.make_async_remote_copy(
            src_ref=var_sent.at[owner], dst_ref=var_received.at[gz],
            send_sem=var_send_sem.at[k], recv_sem=var_sem.at[WORKERS - k],
            device_id=(gx, gy, owner), device_id_type=MESH)

    def exchange_in(k):
        source = lax.rem(gz + k, WORKERS)
        return pltpu.make_async_remote_copy(
            src_ref=sent.at[source], dst_ref=received.at[source],
            send_sem=exchange_send_sem.at[k], recv_sem=exchange_sem.at[k],
            device_id=(gx, gy, source), device_id_type=MESH)

    def var_exchange_in(k):
        source = lax.rem(gz + k, WORKERS)
        return pltpu.make_async_remote_copy(
            src_ref=var_sent.at[source], dst_ref=var_received.at[source],
            send_sem=var_send_sem.at[k], recv_sem=var_sem.at[k],
            device_id=(gx, gy, source), device_id_type=MESH)

    compress(lax.rem(gz + 1, WORKERS))
    pl.semaphore_wait(barrier, len(greeted))

    @pl.loop(1, WORKERS)
    def _(k):
        compress(lax.rem(gz + k + 1, WORKERS))
        exchange(k).start()
        var_exchange(k).start()

    received[gz] = sent[gz]
    var_received[gz] = var_sent[gz]

    @pl.loop(1, WORKERS)
    def _(k):
        exchange_in(k).wait_recv()
        var_exchange_in(k).wait_recv()

    mine = block_index(me)
    for pair in range(WORKERS // 2):
        cols = pl.ds(pair * 2 * PIECE, 2 * PIECE)
        total = received[0, :, cols].astype(jnp.float32)
        for k in range(1, WORKERS):
            total = total + received[k, :, cols].astype(jnp.float32)
        new_momentum = total / WORKERS
        owned = jnp.concatenate(
            [var_received[2 * pair].astype(jnp.float32), var_received[2 * pair + 1].astype(jnp.float32)], axis=-1)
        new_master = master_ref[:, cols] - learning_rate * new_momentum / (jnp.sqrt(owned) + epsilon)
        new_momentum_ref[:, cols] = new_momentum
        new_master_ref[:, cols] = new_master
        w[me["z"] // 2, me["c"], me["y"], me["z"] % 2, me["x"], :, cols] = new_master.astype(jnp.bfloat16)

    def put(src, to, sem):
        pltpu.make_async_remote_copy(
            src_ref=src, dst_ref=src, send_sem=send_sem, recv_sem=sem, device_id=device(to), device_id_type=MESH).start()

    def arrived(dst, sem):
        pltpu.make_async_remote_copy(
            src_ref=dst, dst_ref=dst, send_sem=send_sem, recv_sem=sem, device_id=device(partner), device_id_type=MESH).wait_recv()

    def relay(src):
        pltpu.make_async_remote_copy(
            src_ref=src, dst_ref=src, send_sem=relay_send_sem, recv_sem=relay_sem,
            device_id=device(partner), device_id_type=MESH).start()

    colors = range(3)

    for c in colors:
        for by in (1, 3, 2):
            put(unit(w, me, c), moved(me, DIMS[c][0], by), gather_sem.at[c, by - 1])

    for c in colors:
        for by in (1, 3, 2):
            arrived(unit(w, moved(me, DIMS[c][0], -by), c), gather_sem.at[c, by - 1])

    def spread(c, dim, src, at):
        put(src, moved(me, dim, 1), gather_sem.at[c, at])
        put(src, moved(me, dim, 3), gather_sem.at[c, at + 1])

    def onward(c, dim, p, direction, at):
        half = 0 if direction == 1 else 1
        put(line(w, p, c, half), moved(me, dim, direction), gather_sem.at[c, at + 2 + half])

    def source(dim, by, p=me):
        return moved(p, dim, -by)

    SECOND = 3
    THIRD = (7, 11, 15, 19)
    BY = (0, 1, 3, 2)

    for c in colors:
        spread(c, DIMS[c][1], line(w, me, c), SECOND)
    for c in colors:
        spread(c, DIMS[c][2], line(w, me, c), THIRD[0])
        relay(line(w, me, c))

    def third(c, i):
        p = source(DIMS[c][1], BY[i])
        spread(c, DIMS[c][2], line(w, p, c), THIRD[i])

    for j, by in enumerate((1, 3)):
        for c in colors:
            p = source(DIMS[c][1], by)
            arrived(line(w, p, c), gather_sem.at[c, SECOND + j])
            onward(c, DIMS[c][1], p, by, SECOND)
    for i in (1, 2):
        for c in colors:
            third(c, i)
            relay(line(w, source(DIMS[c][1], BY[i]), c))

    def third_near(i):
        for j, by in enumerate((1, 3)):
            for c in colors:
                p = source(DIMS[c][2], by, source(DIMS[c][1], BY[i]))
                arrived(line(w, p, c), gather_sem.at[c, THIRD[i] + j])
                onward(c, DIMS[c][2], p, by, THIRD[i])
                relay(line(w, p, c))

    def third_far(i):
        for c in colors:
            p = source(DIMS[c][2], 2, source(DIMS[c][1], BY[i]))
            for half in (0, 1):
                arrived(line(w, p, c, half), gather_sem.at[c, THIRD[i] + 2 + half])
            relay(line(w, p, c))

    third_near(0)
    for c in colors:
        p = source(DIMS[c][1], 2)
        for half in (0, 1):
            arrived(line(w, p, c, half), gather_sem.at[c, SECOND + 2 + half])
        third(c, 3)
        relay(line(w, p, c))
    third_near(1)
    third_far(0)
    third_near(2)
    third_far(1)
    third_near(3)
    third_far(2)
    third_far(3)

    theirs = w.at[:, partner["c"]]
    pltpu.make_async_remote_copy(
        src_ref=theirs, dst_ref=theirs, send_sem=relay_send_sem, recv_sem=relay_sem,
        device_id=device(partner), device_id_type=MESH).wait()
    ours = w.at[:, me["c"]]
    drained = [ours.at[0], ours.at[1, pl.ds(0, 3)], ours.at[1, 3, 0], ours.at[1, 3, 1, pl.ds(0, 3)]]
    for part in drained:
        pltpu.make_async_remote_copy(
            src_ref=part, dst_ref=part, send_sem=send_sem, recv_sem=relay_sem,
            device_id=device(partner), device_id_type=MESH).wait_send()

    @pl.loop(1, WORKERS)
    def _(k):
        exchange(k).wait_send()
        var_exchange(k).wait_send()


def put_out(w, new_master, new_momentum, error, w_out, new_master_out, new_momentum_out, error_out, sem):
    pairs = ((w, w_out), (new_master, new_master_out), (new_momentum, new_momentum_out), (error, error_out))
    copies = []
    for i in range(8):
        rows = pl.ds(i * 256, 256)
        copies.append(pltpu.make_async_copy(w.at[rows], w_out.at[rows], sem.at[i]))
    for i, (a, b) in enumerate(pairs[1:]):
        copies.append(pltpu.make_async_copy(a, b, sem.at[8 + i]))
    for copy in copies:
        copy.start()
    for copy in copies:
        copy.wait()


def shards(grads, momentum, variance, master):
    f32 = jnp.float32
    vmem = pl.BlockSpec(memory_space=pltpu.VMEM)
    w, new_master, new_momentum, error = pl.pallas_call(
        step_kernel,
        out_shape=(
            pltpu.VMEM((2, 2, 4, 2, 4, ROWS, WIDTH), jnp.bfloat16),
            pltpu.VMEM((ROWS, WIDTH), f32),
            pltpu.VMEM((ROWS, WIDTH), f32),
            pltpu.VMEM((BLOCKS, WIDTH), f32),
        ),
        in_specs=[vmem] * 4,
        out_specs=(vmem,) * 4,
        scratch_shapes=[
            pltpu.VMEM((WORKERS, ROWS, WIDTH), jnp.bfloat16),
            pltpu.VMEM((WORKERS, ROWS, WIDTH), jnp.bfloat16),
            pltpu.VMEM((WORKERS, ROWS, PIECE), jnp.bfloat16),
            pltpu.VMEM((WORKERS, ROWS, PIECE), jnp.bfloat16),
            pltpu.SemaphoreType.DMA,
            pltpu.SemaphoreType.DMA((WORKERS,)),
            pltpu.SemaphoreType.DMA((WORKERS,)),
            pltpu.SemaphoreType.DMA((3, 23)),
            pltpu.SemaphoreType.DMA,
            pltpu.SemaphoreType.DMA,
            pltpu.SemaphoreType.DMA((WORKERS,)),
            pltpu.SemaphoreType.DMA((WORKERS,)),
        ],
        compiler_params=pltpu.CompilerParams(collective_id=0, has_side_effects=True, vmem_limit_bytes=36 << 20),
        name="step",
    )(grads, momentum, variance.T, master)
    w = w.reshape(BLOCKS * ROWS, WIDTH)
    anywhere = pl.BlockSpec(memory_space=pl.ANY)
    hbm = pl.BlockSpec(memory_space=pltpu.HBM)
    weights, new_master, new_momentum, error = pl.pallas_call(
        put_out,
        out_shape=(
            jax.ShapeDtypeStruct((BLOCKS * ROWS, WIDTH), jnp.bfloat16),
            jax.ShapeDtypeStruct((ROWS, WIDTH), f32),
            jax.ShapeDtypeStruct((ROWS, WIDTH), f32),
            jax.ShapeDtypeStruct((BLOCKS, WIDTH), f32),
        ),
        in_specs=[vmem] * 4,
        out_specs=(hbm,) * 4,
        scratch_shapes=[pltpu.SemaphoreType.DMA((11,))],
        compiler_params=pltpu.CompilerParams(vmem_limit_bytes=1 << 20),
        name="put_out",
    )(w, new_master, new_momentum, error)
    return weights, new_master, new_momentum, error[None]


def solution(mesh):
    return jax.shard_map(
        shards,
        mesh=mesh,
        in_specs=(
            P("gz", ("gx", "gy"), None),
            P(("gx", "gy"), None),
            P(("gx", "gy"), "gz"),
            P(("gx", "gy", "gz"), None),
        ),
        out_specs=(
            P(),
            P(("gx", "gy", "gz"), None),
            P(("gx", "gy", "gz"), None),
            P("gz", ("gx", "gy"), None),
        ),
        check_vma=False,
    )
```

time: 190 us -> 71.2 us (0.37)
  waiting for transfers between devices: 116 us -> 0 us
  Pallas kernels: 0 us -> 67.2 us
  local copies, waits for them, and re-layouts: 23.2 us -> 3.05 us
  blocking collectives: 17.1 us -> 0 us
  between operations: 14.1 us -> 0.65 us
  starting transfers between devices: 11.4 us -> 0 us
  other arithmetic: 7.75 us -> 0 us
    all_gather x1 -> x0, waiting for transfers between devices: 102 us -> none  [shards(): weights = lax.all_gather(gathered, ('gx', 'gy'), axis=0, tiled=True)]
    pallas_call x0 -> x2, Pallas kernels: none -> 67.2 us  [the longest x1 61.2 us: shards(): pl.pallas_call(step_kernel, out_shape=(pltpu.VMEM((2, 2, 4, 2, 4, ROWS, W...]
    unnamed x11 -> x6, local copies, waits for them, and re-layouts: 22.3 us -> 3.05 us
    all_to_all x1 -> x0, blocking collectives: 17.1 us -> none  [from_everyone(): return lax.all_to_all(copies, axis, split_axis=0, concat_axis=0, tiled=True)]
    all_to_all x2 -> x0, waiting for transfers between devices: 14 us -> none  [the longest x1 14 us: shards(): lax.all_to_all(compressed[:, None, :], 'gz', split_axis=0, concat_axis=1,...]
    all_to_all x2 -> x0, starting transfers between devices: 11.3 us -> none  [the longest x1 6.19 us: shards(): lax.all_to_all(variance.astype(jnp.bfloat16), 'gz', split_axis=0, concat_...]
    broadcast_in_dim x2 -> x0, other arithmetic: 4.54 us -> none  [the longest x1 2.48 us: shards(): compressed[:, None, :]]
    reduce_sum x2 -> x0, other arithmetic: 2.32 us -> none  [the longest x1 2.22 us: shards(): jnp.mean(jnp.abs(corrected), axis=-1, keepdims=True).astype(jnp.bfloat16)]
  transfers between devices with their start and end apart: 3 -> 0, of which waited for: 2 -> 0; matrix products, arithmetic and copies ran while one was open for 5% -> 0% of each run, Pallas kernels for 0% -> 0%
where the time goes in v1:
time: 71.2 us; the launch traced here: 70.9 us
  Pallas kernels  67.2 us (94%)
  local copies, waits for them, and re-layouts  3.05 us (4%)
    pallas_call x1, Pallas kernels, shards(): pl.pallas_call(step_kernel, out_shape=(pltpu.VMEM((2, 2, 4, 2, 4, ROWS, W...  61.2 us
    pallas_call x1, Pallas kernels, shards(): pl.pallas_call(put_out, out_shape=(jax.ShapeDtypeStruct((BLOCKS * ROWS, W...  6.04 us
    unnamed x6, local copies, waits for them, and re-layouts  3.05 us

profile of v1, /device:TPU:1, one launch (start us, length us, event | category | flops | bytes accessed | tf_op | source)
XLA Modules:
  0.0 70.9 jit_solution(5414183327930955215)
XLA Ops:
  0.6 0.0 copy-start
  0.6 1.2 %copy-done = bf16[1,128,3584]{2,1,0:T(8,128)(2,1)S(1)} copy-done((bf16[1,128,3584]{2,1,0:T(8,128)(2,1)S(1)}, bf16[1,128,3584]{2,1,0:T(8,128)(2,1)}, u32[]{:S(2)}) %copy-start) | copy-done | bytes 917528
  1.8 0.0 copy-start.1
  1.8 0.9 %copy-done.1 = f32[128,448]{0,1:T(8,128)S(1)} copy-done((f32[128,448]{0,1:T(8,128)S(1)}, f32[128,448]{0,1:T(8,128)}, u32[]{:S(2)}) %copy-start.1) | copy-done | bytes 229400
  2.8 0.0 copy-start.2
  2.8 0.9 %copy-done.2 = f32[16,3584]{1,0:T(8,128)S(1)} copy-done((f32[16,3584]{1,0:T(8,128)S(1)}, f32[16,3584]{1,0:T(8,128)}, u32[]{:S(2)}) %copy-start.2) | copy-done | bytes 229400
  3.7 61.2 %step.1 = (bf16[2,2,4,2,4,16,3584]{6,5,4,3,2,1,0:T(8,128)(2,1)S(1)}, f32[16,3584]{1,0:T(8,128)S(1)}, f32[16,3584]{1,0:T(8,128)S(1)}, f32[128,3584]{1,0:T(8,128)S(1)}) custom-call(bf16[1,128,3584]{2,1,0:T(8,128)(2,1)S(1)} %copy-done, f32[128,3584]{1,0:T(8,128)} %m_ref.1, f32[448,128]{1,0:T(8,128)S(1)} %bitcast.4, f32[16,3584]{1,0:T(8,128)S(1)} %copy-done.2), custom_call_target="tpu_custom_call" | custom-call | tf_op jit(solution)/shard_map/step/pallas_call | solution.py:269
  64.9 6.0 %put_out.1 = (bf16[2048,3584]{1,0:T(8,128)(2,1)}, f32[16,3584]{1,0:T(8,128)}, f32[16,3584]{1,0:T(8,128)}, f32[128,3584]{1,0:T(8,128)}) custom-call(bf16[2048,3584]{1,0:T(8,128)(2,1)S(1)} %bitcast.3, f32[16,3584]{1,0:T(8,128)S(1)} %get-tuple-element.13.new_master, f32[16,3584]{1,0:T(8,128)S(1)} %get-tuple-element.14.new_momentum, ...), custom_call_target="tpu_custom_call" | custom-call | tf_op jit(solution)/shard_map/put_out/pallas_call | solution.py:299
Async XLA Ops:
  0.6 1.2 %copy-start = (bf16[1,128,3584]{2,1,0:T(8,128)(2,1)S(1)}, bf16[1,128,3584]{2,1,0:T(8,128)(2,1)}, u32[]{:S(2)}) copy-start(bf16[1,128,3584]{2,1,0:T(8,128)(2,1)} %g_ref.1) | copy-start | bytes 2752516
  1.8 0.9 %copy-start.1 = (f32[128,448]{0,1:T(8,128)S(1)}, f32[128,448]{0,1:T(8,128)}, u32[]{:S(2)}) copy-start(f32[128,448]{0,1:T(8,128)} %param.6) | copy-start | bytes 688132
  2.8 0.9 %copy-start.2 = (f32[16,3584]{1,0:T(8,128)S(1)}, f32[16,3584]{1,0:T(8,128)}, u32[]{:S(2)}) copy-start(f32[16,3584]{1,0:T(8,128)} %master_ref.1) | copy-start | bytes 688132

commit v2 on v0

v2 whole, which is shorter than its diff:
```python
import jax
import jax.numpy as jnp
from jax import lax
from jax.experimental import pallas as pl
from jax.experimental.pallas import tpu as pltpu
from jax.sharding import PartitionSpec as P

beta_one = 0.9
learning_rate = 0.25
epsilon = 1e-08

MESH = pl.DeviceIdType.MESH
WORKERS = 8
ROWS = 16
WIDTH = 3584
PIECE = WIDTH // WORKERS
OTHERS = WORKERS - 1
BLOCKS = 128

DIMS = (("z", "x", "y"), ("x", "y", "z"), ("y", "z", "x"))
COLUMNS = ((0, 1280), (1280, 1152), (2432, 1152))
LONG = ()
ORDER = (
    ("e", 0), ("e", 2), ("e", 1), ("own", 0), ("p1", 0), ("own", 2), ("p1", 2), ("s0", 0), ("s0", 2), ("su", 0, 3),
    ("t00", 0), ("tu", 0, 3), ("own", 1), ("p1", 1), ("su", 0, 1), ("tu", 0, 1), ("s0", 1), ("tu", 0, 2),
    ("su", 0, 2), ("su", 2, 1), ("su", 2, 3), ("tu", 2, 2), ("su", 2, 2), ("t00", 2), ("tu", 2, 1), ("t00", 1),
    ("su", 1, 1), ("tu", 2, 3), ("su", 1, 3), ("su", 1, 2), ("tu", 1, 1), ("t", 0, 1, 1), ("r", 0, "t0", 1, 1),
    ("r", 0, "t0", 3, 0), ("tu", 1, 2), ("tu", 1, 3), ("sf", 2, 1), ("sf", 0, 3), ("sf", 0, 1), ("t", 2, 1, 1),
    ("sf", 2, 3), ("t", 0, 2, 1), ("t", 2, 2, 0), ("t", 1, 2, 0), ("tf", 2, 0, 3), ("sf", 1, 1), ("t", 1, 1, 0),
    ("sf", 1, 3), ("t", 0, 2, 0), ("t", 0, 1, 0), ("t", 2, 2, 1), ("t", 1, 1, 1), ("tf", 2, 0, 1), ("t", 0, 3, 0),
    ("r", 2, "t0", 1, 1), ("r", 2, "t0", 3, 0), ("r", 1, "t0", 1, 1), ("r", 1, "t0", 3, 0), ("r", 0, "t1", 1, 1),
    ("tf", 0, 2, 3), ("t", 1, 2, 1), ("t", 1, 3, 1), ("r", 0, "t2", 1, 1), ("r", 2, "t1", 1, 1), ("t", 0, 3, 1),
    ("t", 2, 1, 0), ("t", 1, 3, 0), ("r", 1, "t2", 3, 0), ("tf", 1, 1, 1), ("r", 2, "t2", 3, 0), ("t", 2, 3, 0),
    ("t", 2, 3, 1), ("tf", 1, 1, 3), ("r", 1, "t1", 3, 0), ("r", 0, "t2", 3, 0), ("r", 2, "t0", "far", 1),
    ("r", 2, "t2", 1, 1), ("tf", 1, 0, 3), ("tf", 0, 2, 1), ("tf", 2, 2, 3), ("r", 1, "t1", 1, 1), ("tf", 2, 1, 1),
    ("r", 2, "t0", "far", 0), ("r", 0, "t1", 3, 0), ("r", 1, "t2", 1, 1), ("tf", 0, 0, 3), ("tf", 2, 2, 1),
    ("tf", 1, 2, 1), ("tf", 2, 1, 3), ("tf", 0, 0, 1), ("tf", 1, 3, 3), ("r", 2, "t1", 3, 0), ("r", 0, "t3", 3, 0),
    ("tf", 1, 0, 1), ("tf", 0, 3, 1), ("tf", 0, 1, 3), ("tf", 2, 3, 3), ("r", 1, "t3", 1, 1), ("r", 2, "t3", 3, 0),
    ("r", 0, "t3", 1, 1), ("r", 0, "t2", "far", 1), ("r", 1, "t3", 3, 0), ("tf", 1, 3, 1), ("tf", 0, 3, 3),
    ("r", 2, "t3", 1, 1), ("tf", 2, 3, 1), ("tf", 1, 2, 3), ("tf", 0, 1, 1), ("r", 0, "t2", "far", 0),
    ("r", 1, "t1", "far", 1), ("r", 1, "t1", "far", 0), ("r", 2, "t2", "far", 1), ("r", 2, "t1", "far", 0),
    ("r", 0, "t0", "far", 0), ("r", 0, "t0", "far", 1), ("r", 1, "t0", "far", 1), ("r", 1, "t2", "far", 0),
    ("r", 2, "t1", "far", 1), ("r", 2, "t2", "far", 0), ("r", 0, "t3", "far", 0), ("r", 0, "t1", "far", 1),
    ("r", 1, "t3", "far", 1), ("r", 1, "t0", "far", 0), ("r", 2, "t3", "far", 1), ("r", 2, "t3", "far", 0),
    ("r", 1, "t2", "far", 1), ("r", 1, "t3", "far", 0), ("r", 0, "t1", "far", 0), ("r", 0, "t3", "far", 1),
)
LINES = ("s", "t0", "t1", "t2", "t3")


def device(p):
    return ((p["z"] // 2) * 2 + p["c"], p["y"], (p["z"] % 2) * 4 + p["x"])


def far(p, dim):
    return {**p, dim: lax.rem(p[dim] + 2, 4)}


def step(p, dim, dr):
    if dim != "z":
        return {**p, dim: lax.rem(p[dim] + dr, 4)}
    low = lax.rem(p["z"], 2)
    return {**p, dim: lax.rem(p["z"] + (5 - 2 * low if dr == 1 else 3 + 2 * low), 4)}


def back(p, dim, dr):
    return step(p, dim, 4 - dr) if dim != "z" else step(p, dim, dr)


def cols(c):
    return pl.ds(*COLUMNS[c])


def line(w, p, c, half):
    first = DIMS[c][0]
    zh, zl = p["z"] // 2, lax.rem(p["z"], 2)
    part = pl.ds(half * 2, 2)
    if first == "x":
        return w.at[zh, p["c"], p["y"], zl, part, :, cols(c)]
    if first == "y":
        return w.at[zh, p["c"], part, zl, p["x"], :, cols(c)]
    return w.at[half, p["c"], p["y"], :, p["x"], :, cols(c)]


def unit(w, p, c):
    return w.at[p["z"] // 2, p["c"], p["y"], lax.rem(p["z"], 2), p["x"], :, cols(c)]


def step_kernel(
    g_hbm, m_hbm, v_hbm, master_hbm,
    w, new_master_ref, new_momentum_ref, error_ref,
    g_ref, m_ref, v_ref, master_ref, sent, received, var_sent, var_received, scale,
    load_sem, exchange_sem, exchange_send_sem, var_sem, gather_sem, send_sem, relay_sem, relay_send_sem,
):
    gx, gy, gz = lax.axis_index("gx"), lax.axis_index("gy"), lax.axis_index("gz")
    me = {"x": lax.rem(gz, 4), "y": gy, "z": (gx // 2) * 2 + gz // 4, "c": lax.rem(gx, 2)}
    partner = {**me, "c": 1 - me["c"]}

    barrier = pltpu.get_barrier_semaphore()
    greeted = [(gx, gy, lax.rem(gz + k, WORKERS)) for k in range(1, WORKERS)]
    greeted += [device({**me, "y": lax.rem(gy + k, 4)}) for k in (1, 2, 3)]
    greeted += [device(step(me, "z", 3)), device(far(me, "z")), device(partner)]
    for d in greeted:
        pl.semaphore_signal(barrier, inc=1, device_id=d, device_id_type=MESH)

    def rows_of(owner):
        return pl.ds(pl.multiple_of(owner * ROWS, ROWS), ROWS)

    def loads(k):
        rows = rows_of(lax.rem(gz + k + 1, WORKERS))
        return (
            pltpu.make_async_copy(g_hbm.at[0, rows, :], g_ref.at[rows, :], load_sem.at[0, k]),
            pltpu.make_async_copy(m_hbm.at[rows, :], m_ref.at[rows, :], load_sem.at[1, k]),
        )

    load_var = pltpu.make_async_copy(v_hbm, v_ref, load_sem.at[2, 0])
    load_master = pltpu.make_async_copy(master_hbm, master_ref, load_sem.at[2, 1])
    load_var.start()

    @pl.loop(0, WORKERS)
    def _(k):
        for copy in loads(k):
            copy.start()

    load_master.start()

    load_var.wait()
    var = v_ref[...].T.astype(jnp.bfloat16)
    for k in range(WORKERS):
        var_sent[k] = var[k * ROWS:(k + 1) * ROWS, :]

    @pl.loop(0, WORKERS)
    def _(k):
        for copy in loads(k):
            copy.wait()
        owner = lax.rem(gz + k + 1, WORKERS)
        rows = rows_of(owner)
        corrected = beta_one * m_ref[rows, :] + (1.0 - beta_one) * g_ref[rows, :].astype(jnp.float32)
        level = jnp.mean(jnp.abs(corrected), axis=-1, keepdims=True).astype(jnp.bfloat16).astype(jnp.float32)
        compressed = jnp.where(corrected >= 0.0, level, -level)
        sent[owner] = compressed.astype(jnp.bfloat16)
        error_ref[rows, :] = corrected - compressed

    pl.semaphore_wait(barrier, len(greeted))

    def to_owner(k, src, dst, sems):
        owner = lax.rem(gz + k, WORKERS)
        pltpu.make_async_remote_copy(
            src_ref=src.at[owner, :, sems[2]], dst_ref=dst.at[gz, :, sems[2]], send_sem=sems[0], recv_sem=sems[1],
            device_id=(gx, gy, owner), device_id_type=MESH).start()

    def of_all(ref, sems):
        return pltpu.make_async_remote_copy(
            src_ref=ref.at[pl.ds(0, OTHERS), :, sems[2]], dst_ref=ref.at[pl.ds(0, OTHERS), :, sems[2]],
            send_sem=sems[0], recv_sem=sems[1], device_id=device(partner), device_id_type=MESH)

    var_sems = (var_sem.at[0], var_sem.at[1], slice(None))
    for k in range(1, WORKERS):
        to_owner(k, var_sent, var_received, var_sems)

    def exchange_sems(c):
        return (exchange_send_sem.at[c], exchange_sem.at[c], cols(c))

    def sem_of(nm, c, dr, half=None):
        if nm == "p1":
            return gather_sem.at[c, dr - 1]
        at = 3 + 6 * LINES.index(nm)
        return gather_sem.at[c, at + ((4 if dr == "far" else dr - 1) + half)]

    def send(src, to, sem):
        pltpu.make_async_remote_copy(
            src_ref=src, dst_ref=src, send_sem=send_sem, recv_sem=sem, device_id=device(to), device_id_type=MESH).start()

    def relay(src):
        pltpu.make_async_remote_copy(
            src_ref=src, dst_ref=src, send_sem=relay_send_sem, recv_sem=relay_sem,
            device_id=device(partner), device_id_type=MESH).start()

    def came_from(nm, c, dr):
        first, second, third = DIMS[c]
        if nm == "p1":
            return far(me, first) if dr == 2 else back(me, first, dr)
        if nm == "s":
            return far(me, second) if dr == "far" else back(me, second, dr)
        i = int(nm[1])
        p = (me, back(me, second, 1), back(me, second, 3), far(me, second))[i]
        return far(p, third) if dr == "far" else back(p, third, dr)

    def contents(nm, c, dr, half=None):
        p = came_from(nm, c, dr)
        return unit(w, p, c) if nm == "p1" else line(w, p, c, half)

    done = set()
    fresh = []

    def wait(nm, c, dr, half=None):
        if (nm, c, dr, half) in done:
            return
        done.add((nm, c, dr, half))
        held = contents(nm, c, dr, half)
        pltpu.make_async_remote_copy(
            src_ref=held, dst_ref=held, send_sem=send_sem, recv_sem=sem_of(nm, c, dr, half),
            device_id=device(partner), device_id_type=MESH).wait_recv()
        fresh.append(held)

    def send_unit(c, p, nm):
        dim = DIMS[c][1 if nm == "s" else 2]
        half = p[DIMS[c][0]] // 2
        for dr in (1, 3):
            send(unit(w, p, c), step(me, dim, dr), sem_of(nm, c, dr, half))

    def send_onward(c, dim, nm, dr):
        if dim == "z" and (nm, c) in LONG:
            halves = (0, 1) if dr == 1 else ()
        else:
            halves = (0,) if dr == 1 else (1,)
        for half in halves:
            wait(nm, c, dr, half)
        for half in halves:
            send(contents(nm, c, dr, half), step(me, dim, 4 - dr if dim == "z" else dr), sem_of(nm, c, "far", half))

    def update_scale():
        received[gz] = sent[gz]
        var_received[gz] = var_sent[gz]
        of_all(var_received, var_sems).wait_recv()
        for pair in range(WORKERS // 2):
            owned = jnp.concatenate(
                [var_received[2 * pair].astype(jnp.float32), var_received[2 * pair + 1].astype(jnp.float32)], axis=-1)
            scale[:, pl.ds(pair * 2 * PIECE, 2 * PIECE)] = jnp.sqrt(owned) + epsilon
        load_master.wait()

    def update(c):
        of_all(received, exchange_sems(c)).wait_recv()
        total = received[0, :, cols(c)].astype(jnp.float32)
        for k in range(1, WORKERS):
            total = total + received[k, :, cols(c)].astype(jnp.float32)
        new_momentum = total / WORKERS
        new_master = master_ref[:, cols(c)] - learning_rate * new_momentum / scale[:, cols(c)]
        w[me["z"] // 2, me["c"], me["y"], lax.rem(me["z"], 2), me["x"], :, cols(c)] = new_master.astype(jnp.bfloat16)
        new_momentum_ref[:, cols(c)] = new_momentum
        new_master_ref[:, cols(c)] = new_master

    updated = []
    for task in ORDER:
        kind, c = task[0], task[1]
        first, second, third = DIMS[c]
        if kind == "e":
            for k in range(1, WORKERS):
                to_owner(k, sent, received, exchange_sems(c))
        elif kind == "own":
            if not updated:
                update_scale()
            updated.append(c)
            update(c)
            fresh.append(unit(w, me, c))
        elif kind == "p1":
            for dr in (1, 3):
                send(unit(w, me, c), step(me, first, dr), sem_of("p1", c, dr))
            send(unit(w, me, c), far(me, first), sem_of("p1", c, 2))
        elif kind in ("s0", "t00"):
            send_unit(c, me, kind[:-1])
        elif kind in ("su", "tu"):
            wait("p1", c, task[2])
            send_unit(c, came_from("p1", c, task[2]), "s" if kind == "su" else "t0")
        elif kind == "sf":
            send_onward(c, second, "s", task[2])
        elif kind == "t":
            i, half = task[2:]
            dr = (1, 3, "far")[i - 1]
            wait("s", c, dr, half)
            for way in (1, 3):
                send(contents("s", c, dr, half), step(me, third, way), sem_of("t%d" % i, c, way, half))
        elif kind == "tf":
            send_onward(c, third, "t%d" % task[2], task[3])
        else:
            wait(task[2], c, *task[3:])
        if kind not in ("own", "p1", "s0"):
            for held in fresh:
                relay(held)
            fresh.clear()

    theirs = w.at[:, partner["c"]]
    pltpu.make_async_remote_copy(
        src_ref=theirs, dst_ref=theirs, send_sem=relay_send_sem, recv_sem=relay_sem,
        device_id=device(partner), device_id_type=MESH).wait()
    ours = w.at[:, me["c"]]
    for part in (ours.at[0], ours.at[1, pl.ds(0, 3)], ours.at[1, 3, 0], ours.at[1, 3, 1, pl.ds(0, 3)]):
        pltpu.make_async_remote_copy(
            src_ref=part, dst_ref=part, send_sem=send_sem, recv_sem=relay_sem,
            device_id=device(partner), device_id_type=MESH).wait_send()
    of_all(var_sent, var_sems).wait_send()
    for c in range(3):
        of_all(sent, exchange_sems(c)).wait_send()


def put_out(w, new_master, new_momentum, error, w_out, new_master_out, new_momentum_out, error_out, sem):
    copies = []
    for i in range(8):
        rows = pl.ds(i * 256, 256)
        copies.append(pltpu.make_async_copy(w.at[rows], w_out.at[rows], sem.at[i]))
    pairs = ((new_master, new_master_out), (new_momentum, new_momentum_out), (error, error_out))
    for i, (a, b) in enumerate(pairs):
        copies.append(pltpu.make_async_copy(a, b, sem.at[8 + i]))
    for copy in copies:
        copy.start()
    for copy in copies:
        copy.wait()


def shards(grads, momentum, variance, master):
    f32 = jnp.float32
    vmem = pl.BlockSpec(memory_space=pltpu.VMEM)
    hbm = pl.BlockSpec(memory_space=pltpu.HBM)
    w, new_master, new_momentum, error = pl.pallas_call(
        step_kernel,
        out_shape=(
            pltpu.VMEM((2, 2, 4, 2, 4, ROWS, WIDTH), jnp.bfloat16),
            pltpu.VMEM((ROWS, WIDTH), f32),
            pltpu.VMEM((ROWS, WIDTH), f32),
            pltpu.VMEM((BLOCKS, WIDTH), f32),
        ),
        in_specs=[hbm] * 4,
        out_specs=(vmem,) * 4,
        scratch_shapes=[
            pltpu.VMEM((BLOCKS, WIDTH), jnp.bfloat16),
            pltpu.VMEM((BLOCKS, WIDTH), f32),
            pltpu.VMEM((PIECE, BLOCKS), f32),
            pltpu.VMEM((ROWS, WIDTH), f32),
            pltpu.VMEM((WORKERS, ROWS, WIDTH), jnp.bfloat16),
            pltpu.VMEM((WORKERS, ROWS, WIDTH), jnp.bfloat16),
            pltpu.VMEM((WORKERS, ROWS, PIECE), jnp.bfloat16),
            pltpu.VMEM((WORKERS, ROWS, PIECE), jnp.bfloat16),
            pltpu.VMEM((ROWS, WIDTH), f32),
            pltpu.SemaphoreType.DMA((3, WORKERS)),
            pltpu.SemaphoreType.DMA((3,)),
            pltpu.SemaphoreType.DMA((3,)),
            pltpu.SemaphoreType.DMA((2,)),
            pltpu.SemaphoreType.DMA((3, 33)),
            pltpu.SemaphoreType.DMA,
            pltpu.SemaphoreType.DMA,
            pltpu.SemaphoreType.DMA,
        ],
        compiler_params=pltpu.CompilerParams(collective_id=0, has_side_effects=True, vmem_limit_bytes=36 << 20),
        name="step",
    )(grads, momentum, variance.T, master)
    w = w.reshape(BLOCKS * ROWS, WIDTH)
    weights, new_master, new_momentum, error = pl.pallas_call(
        put_out,
        out_shape=(
            jax.ShapeDtypeStruct((BLOCKS * ROWS, WIDTH), jnp.bfloat16),
            jax.ShapeDtypeStruct((ROWS, WIDTH), f32),
            jax.ShapeDtypeStruct((ROWS, WIDTH), f32),
            jax.ShapeDtypeStruct((BLOCKS, WIDTH), f32),
        ),
        in_specs=[vmem] * 4,
        out_specs=(hbm,) * 4,
        scratch_shapes=[pltpu.SemaphoreType.DMA((11,))],
        compiler_params=pltpu.CompilerParams(vmem_limit_bytes=1 << 20),
        name="put_out",
    )(w, new_master, new_momentum, error)
    return weights, new_master, new_momentum, error[None]


def solution(mesh):
    return jax.shard_map(
        shards,
        mesh=mesh,
        in_specs=(
            P("gz", ("gx", "gy"), None),
            P(("gx", "gy"), None),
            P(("gx", "gy"), "gz"),
            P(("gx", "gy", "gz"), None),
        ),
        out_specs=(
            P(),
            P(("gx", "gy", "gz"), None),
            P(("gx", "gy", "gz"), None),
            P("gz", ("gx", "gy"), None),
        ),
        check_vma=False,
    )
```

time: 190 us -> 62.2 us (0.33)
  waiting for transfers between devices: 116 us -> 0 us
  Pallas kernels: 0 us -> 58.3 us
  local copies, waits for them, and re-layouts: 23.2 us -> 3.05 us
  blocking collectives: 17.1 us -> 0 us
  between operations: 14.1 us -> 0.65 us
  starting transfers between devices: 11.4 us -> 0 us
  other arithmetic: 7.75 us -> 0 us
    all_gather x1 -> x0, waiting for transfers between devices: 102 us -> none  [shards(): weights = lax.all_gather(gathered, ('gx', 'gy'), axis=0, tiled=True)]
    pallas_call x0 -> x2, Pallas kernels: none -> 58.3 us  [the longest x1 52.3 us: shards(): pl.pallas_call(step_kernel, out_shape=(pltpu.VMEM((2, 2, 4, 2, 4, ROWS, W...]
    unnamed x11 -> x6, local copies, waits for them, and re-layouts: 22.3 us -> 3.05 us
    all_to_all x1 -> x0, blocking collectives: 17.1 us -> none  [from_everyone(): return lax.all_to_all(copies, axis, split_axis=0, concat_axis=0, tiled=True)]
    all_to_all x2 -> x0, waiting for transfers between devices: 14 us -> none  [the longest x1 14 us: shards(): lax.all_to_all(compressed[:, None, :], 'gz', split_axis=0, concat_axis=1,...]
    all_to_all x2 -> x0, starting transfers between devices: 11.3 us -> none  [the longest x1 6.19 us: shards(): lax.all_to_all(variance.astype(jnp.bfloat16), 'gz', split_axis=0, concat_...]
    broadcast_in_dim x2 -> x0, other arithmetic: 4.54 us -> none  [the longest x1 2.48 us: shards(): compressed[:, None, :]]
    reduce_sum x2 -> x0, other arithmetic: 2.32 us -> none  [the longest x1 2.22 us: shards(): jnp.mean(jnp.abs(corrected), axis=-1, keepdims=True).astype(jnp.bfloat16)]
  transfers between devices with their start and end apart: 3 -> 0, of which waited for: 2 -> 0; matrix products, arithmetic and copies ran while one was open for 5% -> 0% of each run, Pallas kernels for 0% -> 0%
where the time goes in v2:
time: 62.2 us; the launch traced here: 62 us
  Pallas kernels  58.3 us (94%)
  local copies, waits for them, and re-layouts  3.05 us (5%)
  between operations  0.65 us (1%)
    pallas_call x1, Pallas kernels, shards(): pl.pallas_call(step_kernel, out_shape=(pltpu.VMEM((2, 2, 4, 2, 4, ROWS, W...  52.3 us
    pallas_call x1, Pallas kernels, shards(): pl.pallas_call(put_out, out_shape=(jax.ShapeDtypeStruct((BLOCKS * ROWS, W...  6.04 us
    unnamed x6, local copies, waits for them, and re-layouts  3.05 us

profile of v2, /device:TPU:1, one launch (start us, length us, event | category | flops | bytes accessed | tf_op | source)
XLA Modules:
  0.0 62.0 jit_solution(11233356405795552890)
XLA Ops:
  0.6 0.0 copy-start
  0.6 1.2 %copy-done = bf16[1,128,3584]{2,1,0:T(8,128)(2,1)S(1)} copy-done((bf16[1,128,3584]{2,1,0:T(8,128)(2,1)S(1)}, bf16[1,128,3584]{2,1,0:T(8,128)(2,1)}, u32[]{:S(2)}) %copy-start) | copy-done | bytes 917528
  1.8 0.0 copy-start.1
  1.8 0.9 %copy-done.1 = f32[128,448]{0,1:T(8,128)S(1)} copy-done((f32[128,448]{0,1:T(8,128)S(1)}, f32[128,448]{0,1:T(8,128)}, u32[]{:S(2)}) %copy-start.1) | copy-done | bytes 229400
  2.8 0.0 copy-start.2
  2.8 0.9 %copy-done.2 = f32[16,3584]{1,0:T(8,128)S(1)} copy-done((f32[16,3584]{1,0:T(8,128)S(1)}, f32[16,3584]{1,0:T(8,128)}, u32[]{:S(2)}) %copy-start.2) | copy-done | bytes 229400
  3.7 52.3 %step.1 = (bf16[2,2,4,2,4,16,3584]{6,5,4,3,2,1,0:T(8,128)(2,1)S(1)}, f32[16,3584]{1,0:T(8,128)S(1)}, f32[16,3584]{1,0:T(8,128)S(1)}, f32[128,3584]{1,0:T(8,128)S(1)}) custom-call(bf16[1,128,3584]{2,1,0:T(8,128)(2,1)S(1)} %copy-done, f32[128,3584]{1,0:T(8,128)} %m_hbm.1, f32[448,128]{1,0:T(8,128)S(1)} %bitcast.4, f32[16,3584]{1,0:T(8,128)S(1)} %copy-done.2), custom_call_target="tpu_custom_call" | custom-call | tf_op jit(solution)/shard_map/step/pallas_call | solution.py:313
  56.0 6.0 %put_out.1 = (bf16[2048,3584]{1,0:T(8,128)(2,1)}, f32[16,3584]{1,0:T(8,128)}, f32[16,3584]{1,0:T(8,128)}, f32[128,3584]{1,0:T(8,128)}) custom-call(bf16[2048,3584]{1,0:T(8,128)(2,1)S(1)} %bitcast.3, f32[16,3584]{1,0:T(8,128)S(1)} %get-tuple-element.13.new_master, f32[16,3584]{1,0:T(8,128)S(1)} %get-tuple-element.14.new_momentum, ...), custom_call_target="tpu_custom_call" | custom-call | tf_op jit(solution)/shard_map/put_out/pallas_call | solution.py:346
Async XLA Ops:
  0.6 1.2 %copy-start = (bf16[1,128,3584]{2,1,0:T(8,128)(2,1)S(1)}, bf16[1,128,3584]{2,1,0:T(8,128)(2,1)}, u32[]{:S(2)}) copy-start(bf16[1,128,3584]{2,1,0:T(8,128)(2,1)} %g_hbm.1) | copy-start | bytes 2752516
  1.8 0.9 %copy-start.1 = (f32[128,448]{0,1:T(8,128)S(1)}, f32[128,448]{0,1:T(8,128)}, u32[]{:S(2)}) copy-start(f32[128,448]{0,1:T(8,128)} %param.6) | copy-start | bytes 688132
  2.8 0.9 %copy-start.2 = (f32[16,3584]{1,0:T(8,128)S(1)}, f32[16,3584]{1,0:T(8,128)}, u32[]{:S(2)}) copy-start(f32[16,3584]{1,0:T(8,128)} %master_hbm.1) | copy-start | bytes 688132

commit v3 on v2

--- a/solution.py
+++ b/solution.py
@@ -17,32 +17,57 @@
 OTHERS = WORKERS - 1
 BLOCKS = 128
 
-DIMS = (("z", "x", "y"), ("x", "y", "z"), ("y", "z", "x"))
-COLUMNS = ((0, 1280), (1280, 1152), (2432, 1152))
-LONG = ()
+DIMS = (("y", "z", "x"), ("y", "z", "x"), ("x", "z", "y"), ("x", "y", "z"), ("x", "y", "z"), ("x", "z", "y"))
+COLUMNS = ((0, 768), (768, 640), (1408, 640), (2048, 640), (2688, 384), (3072, 512))
+COLORS = len(COLUMNS)
+LONG = (("t2", 4),)
 ORDER = (
-    ("e", 0), ("e", 2), ("e", 1), ("own", 0), ("p1", 0), ("own", 2), ("p1", 2), ("s0", 0), ("s0", 2), ("su", 0, 3),
-    ("t00", 0), ("tu", 0, 3), ("own", 1), ("p1", 1), ("su", 0, 1), ("tu", 0, 1), ("s0", 1), ("tu", 0, 2),
-    ("su", 0, 2), ("su", 2, 1), ("su", 2, 3), ("tu", 2, 2), ("su", 2, 2), ("t00", 2), ("tu", 2, 1), ("t00", 1),
-    ("su", 1, 1), ("tu", 2, 3), ("su", 1, 3), ("su", 1, 2), ("tu", 1, 1), ("t", 0, 1, 1), ("r", 0, "t0", 1, 1),
-    ("r", 0, "t0", 3, 0), ("tu", 1, 2), ("tu", 1, 3), ("sf", 2, 1), ("sf", 0, 3), ("sf", 0, 1), ("t", 2, 1, 1),
-    ("sf", 2, 3), ("t", 0, 2, 1), ("t", 2, 2, 0), ("t", 1, 2, 0), ("tf", 2, 0, 3), ("sf", 1, 1), ("t", 1, 1, 0),
-    ("sf", 1, 3), ("t", 0, 2, 0), ("t", 0, 1, 0), ("t", 2, 2, 1), ("t", 1, 1, 1), ("tf", 2, 0, 1), ("t", 0, 3, 0),
-    ("r", 2, "t0", 1, 1), ("r", 2, "t0", 3, 0), ("r", 1, "t0", 1, 1), ("r", 1, "t0", 3, 0), ("r", 0, "t1", 1, 1),
-    ("tf", 0, 2, 3), ("t", 1, 2, 1), ("t", 1, 3, 1), ("r", 0, "t2", 1, 1), ("r", 2, "t1", 1, 1), ("t", 0, 3, 1),
-    ("t", 2, 1, 0), ("t", 1, 3, 0), ("r", 1, "t2", 3, 0), ("tf", 1, 1, 1), ("r", 2, "t2", 3, 0), ("t", 2, 3, 0),
-    ("t", 2, 3, 1), ("tf", 1, 1, 3), ("r", 1, "t1", 3, 0), ("r", 0, "t2", 3, 0), ("r", 2, "t0", "far", 1),
-    ("r", 2, "t2", 1, 1), ("tf", 1, 0, 3), ("tf", 0, 2, 1), ("tf", 2, 2, 3), ("r", 1, "t1", 1, 1), ("tf", 2, 1, 1),
-    ("r", 2, "t0", "far", 0), ("r", 0, "t1", 3, 0), ("r", 1, "t2", 1, 1), ("tf", 0, 0, 3), ("tf", 2, 2, 1),
-    ("tf", 1, 2, 1), ("tf", 2, 1, 3), ("tf", 0, 0, 1), ("tf", 1, 3, 3), ("r", 2, "t1", 3, 0), ("r", 0, "t3", 3, 0),
-    ("tf", 1, 0, 1), ("tf", 0, 3, 1), ("tf", 0, 1, 3), ("tf", 2, 3, 3), ("r", 1, "t3", 1, 1), ("r", 2, "t3", 3, 0),
-    ("r", 0, "t3", 1, 1), ("r", 0, "t2", "far", 1), ("r", 1, "t3", 3, 0), ("tf", 1, 3, 1), ("tf", 0, 3, 3),
-    ("r", 2, "t3", 1, 1), ("tf", 2, 3, 1), ("tf", 1, 2, 3), ("tf", 0, 1, 1), ("r", 0, "t2", "far", 0),
-    ("r", 1, "t1", "far", 1), ("r", 1, "t1", "far", 0), ("r", 2, "t2", "far", 1), ("r", 2, "t1", "far", 0),
-    ("r", 0, "t0", "far", 0), ("r", 0, "t0", "far", 1), ("r", 1, "t0", "far", 1), ("r", 1, "t2", "far", 0),
-    ("r", 2, "t1", "far", 1), ("r", 2, "t2", "far", 0), ("r", 0, "t3", "far", 0), ("r", 0, "t1", "far", 1),
-    ("r", 1, "t3", "far", 1), ("r", 1, "t0", "far", 0), ("r", 2, "t3", "far", 1), ("r", 2, "t3", "far", 0),
-    ("r", 1, "t2", "far", 1), ("r", 1, "t3", "far", 0), ("r", 0, "t1", "far", 0), ("r", 0, "t3", "far", 1),
+    ("e", 0), ("e", 1), ("e", 2), ("e", 4), ("e", 5), ("e", 3), ("own", 0), ("p1", 0), ("own", 1), ("s0", 0),
+    ("s0", 1), ("p1", 1), ("own", 2), ("s0", 2), ("p1", 2), ("su", 0, 3), ("own", 4), ("t00", 2), ("p1", 4),
+    ("su", 0, 1), ("t00", 4), ("tu", 0, 3), ("tu", 0, 1), ("su", 0, 2), ("su", 1, 1), ("su", 1, 3), ("own", 5),
+    ("p1", 5), ("t00", 1), ("s0", 5), ("su", 1, 2), ("own", 3), ("t00", 3), ("p1", 3), ("s0", 4), ("su", 2, 3),
+    ("tu", 2, 1), ("su", 2, 1), ("tu", 1, 3), ("tu", 2, 3), ("su", 2, 2), ("su", 4, 1), ("t00", 0), ("tu", 1, 1),
+    ("tu", 4, 3), ("tu", 2, 2), ("tu", 4, 1), ("su", 4, 2), ("su", 4, 3), ("sf", 0, 1), ("t00", 5), ("tu", 1, 2),
+    ("su", 5, 3), ("tu", 5, 3), ("su", 5, 1), ("tu", 5, 1), ("tu", 4, 2), ("t", 0, 1, 1), ("s0", 3), ("tu", 0, 2),
+    ("su", 5, 2), ("t", 0, 2, 0), ("t", 1, 1, 1), ("t", 1, 2, 1), ("sf", 1, 3), ("sf", 1, 1), ("t", 1, 1, 0),
+    ("su", 3, 3), ("tu", 5, 2), ("su", 3, 1), ("tu", 3, 3), ("su", 3, 2), ("sf", 2, 3), ("t", 1, 2, 0),
+    ("t", 2, 1, 1), ("sf", 2, 1), ("sf", 0, 3), ("sf", 4, 3), ("r", 2, "t0", 1, 1), ("r", 2, "t0", 3, 0),
+    ("tu", 3, 2), ("sf", 4, 1), ("t", 4, 2, 1), ("t", 4, 1, 0), ("t", 4, 1, 1), ("t", 2, 1, 0), ("t", 2, 2, 0),
+    ("tf", 1, 0, 1), ("tf", 0, 0, 1), ("r", 1, "t0", 1, 1), ("r", 1, "t0", 3, 0), ("r", 0, "t1", 1, 1),
+    ("r", 4, "t0", 1, 1), ("t", 5, 1, 0), ("tf", 5, 0, 1), ("r", 4, "t0", 3, 0), ("r", 0, "t0", 1, 1), ("t", 0, 2, 1),
+    ("r", 0, "t0", 3, 0), ("tf", 5, 0, 3), ("sf", 5, 1), ("t", 0, 1, 0), ("sf", 3, 1), ("r", 5, "t0", 1, 1),
+    ("r", 5, "t0", 3, 0), ("tf", 4, 0, 3), ("t", 4, 2, 0), ("t", 1, 3, 1), ("t", 0, 3, 0), ("r", 0, "t2", 3, 0),
+    ("t", 5, 1, 1), ("sf", 3, 3), ("t", 5, 2, 1), ("t", 3, 1, 1), ("tf", 4, 2, 3), ("t", 1, 3, 0), ("t", 5, 2, 0),
+    ("tf", 1, 1, 3), ("t", 2, 3, 1), ("sf", 5, 3), ("t", 3, 2, 0), ("tf", 0, 1, 3), ("t", 3, 1, 0), ("t", 2, 3, 0),
+    ("r", 1, "t1", 1, 1), ("t", 4, 3, 1), ("r", 2, "t1", 1, 1), ("t", 3, 2, 1), ("tu", 3, 1), ("tf", 0, 2, 1),
+    ("tf", 2, 1, 1), ("r", 1, "t2", 1, 1), ("t", 4, 3, 0), ("tf", 4, 1, 1), ("r", 4, "t2", 3, 1),
+    ("r", 2, "t1", 3, 0), ("r", 1, "t1", 3, 0), ("r", 4, "t1", 3, 0), ("t", 5, 3, 0), ("r", 2, "t2", 3, 0),
+    ("r", 1, "t2", 3, 0), ("t", 3, 3, 0), ("r", 4, "t1", 1, 1), ("r", 5, "t1", 3, 0), ("r", 1, "t0", "far", 0),
+    ("r", 4, "t0", "far", 1), ("r", 4, "t2", 3, 0), ("r", 5, "t0", "far", 0), ("r", 5, "t0", "far", 1),
+    ("t", 3, 3, 1), ("r", 0, "t0", "far", 0), ("r", 0, "t1", 3, 0), ("r", 3, "t1", 1, 1), ("t", 0, 3, 1),
+    ("tf", 5, 1, 1), ("t", 5, 3, 1), ("tf", 1, 3, 3), ("tf", 4, 2, 1), ("tf", 1, 2, 3), ("tf", 3, 1, 3),
+    ("tf", 0, 2, 3), ("r", 5, "t1", 1, 1), ("t", 2, 2, 1), ("r", 3, "t2", 3, 0), ("r", 0, "t2", 1, 1),
+    ("tf", 5, 2, 3), ("tf", 2, 3, 3), ("r", 5, "t2", 1, 1), ("r", 3, "t1", 3, 0), ("r", 0, "t3", 3, 0),
+    ("r", 5, "t2", 3, 0), ("tf", 3, 1, 1), ("tf", 3, 2, 3), ("tf", 0, 1, 1), ("tf", 4, 1, 3), ("tf", 5, 2, 1),
+    ("r", 1, "t3", 1, 1), ("tf", 2, 0, 3), ("r", 1, "t3", 3, 0), ("tf", 1, 2, 1), ("tf", 2, 3, 1),
+    ("r", 2, "t3", 1, 1), ("r", 4, "t3", 1, 1), ("tf", 3, 0, 3), ("tf", 1, 0, 3), ("tf", 0, 0, 3),
+    ("r", 3, "t0", 3, 0), ("tf", 3, 0, 1), ("r", 1, "t1", "far", 1), ("r", 2, "t3", 3, 0), ("r", 4, "t3", 3, 0),
+    ("tf", 5, 1, 3), ("tf", 4, 3, 1), ("r", 3, "t2", 1, 1), ("r", 4, "t1", "far", 0), ("r", 3, "t0", 1, 1),
+    ("r", 5, "t3", 3, 0), ("tf", 0, 3, 1), ("tf", 2, 0, 1), ("r", 0, "t1", "far", 1), ("tf", 2, 2, 1),
+    ("tf", 5, 3, 3), ("r", 2, "t1", "far", 0), ("tf", 5, 3, 1), ("tf", 3, 2, 1), ("tf", 4, 0, 1), ("tf", 1, 1, 1),
+    ("tf", 3, 3, 1), ("r", 3, "t3", 3, 0), ("tf", 3, 3, 3), ("r", 0, "t2", "far", 0), ("tf", 4, 3, 3),
+    ("tf", 0, 3, 3), ("tf", 2, 1, 3), ("tf", 2, 2, 3), ("tf", 1, 3, 1), ("r", 5, "t1", "far", 0),
+    ("r", 1, "t3", "far", 1), ("r", 0, "t3", 1, 1), ("r", 4, "t2", "far", 0), ("r", 3, "t3", 1, 1),
+    ("r", 5, "t3", 1, 1), ("r", 5, "t2", "far", 1), ("r", 4, "t2", "far", 1), ("r", 1, "t2", "far", 1),
+    ("r", 3, "t1", "far", 1), ("r", 2, "t2", 1, 1), ("r", 2, "t3", "far", 1), ("r", 0, "t1", "far", 0),
+    ("r", 3, "t1", "far", 0), ("r", 5, "t2", "far", 0), ("r", 0, "t2", "far", 1), ("r", 3, "t2", "far", 1),
+    ("r", 2, "t0", "far", 1), ("r", 1, "t2", "far", 0), ("r", 3, "t0", "far", 0), ("r", 4, "t1", "far", 1),
+    ("r", 2, "t3", "far", 0), ("r", 5, "t1", "far", 1), ("r", 1, "t0", "far", 1), ("r", 4, "t3", "far", 0),
+    ("r", 0, "t3", "far", 0), ("r", 3, "t0", "far", 1), ("r", 5, "t3", "far", 1), ("r", 2, "t0", "far", 0),
+    ("r", 0, "t0", "far", 1), ("r", 3, "t2", "far", 0), ("r", 1, "t1", "far", 0), ("r", 3, "t3", "far", 1),
+    ("r", 2, "t1", "far", 1), ("r", 4, "t0", "far", 0), ("r", 2, "t2", "far", 0), ("r", 4, "t3", "far", 1),
+    ("r", 1, "t3", "far", 0), ("r", 0, "t3", "far", 1), ("r", 5, "t3", "far", 0), ("r", 2, "t2", "far", 1),
+    ("r", 3, "t3", "far", 0),
 )
 LINES = ("s", "t0", "t1", "t2", "t3")
 
@@ -128,8 +153,27 @@
     for k in range(WORKERS):
         var_sent[k] = var[k * ROWS:(k + 1) * ROWS, :]
 
-    @pl.loop(0, WORKERS)
-    def _(k):
+    pl.semaphore_wait(barrier, len(greeted))
+
+    def to_owner(k, src, dst, sems):
+        owner = lax.rem(gz + k, WORKERS)
+        pltpu.make_async_remote_copy(
+            src_ref=src.at[owner, :, sems[2]], dst_ref=dst.at[gz, :, sems[2]], send_sem=sems[0], recv_sem=sems[1],
+            device_id=(gx, gy, owner), device_id_type=MESH).start()
+
+    def of_all(ref, sems):
+        return pltpu.make_async_remote_copy(
+            src_ref=ref.at[pl.ds(0, OTHERS), :, sems[2]], dst_ref=ref.at[pl.ds(0, OTHERS), :, sems[2]],
+            send_sem=sems[0], recv_sem=sems[1], device_id=device(partner), device_id_type=MESH)
+
+    var_sems = (var_sem.at[0], var_sem.at[1], slice(None))
+    for k in range(1, WORKERS):
+        to_owner(k, var_sent, var_received, var_sems)
+
+    def exchange_sems(c):
+        return (exchange_send_sem.at[c], exchange_sem.at[c], cols(c))
+
+    def compress(k):
         for copy in loads(k):
             copy.wait()
         owner = lax.rem(gz + k + 1, WORKERS)
@@ -140,25 +184,12 @@
         sent[owner] = compressed.astype(jnp.bfloat16)
         error_ref[rows, :] = corrected - compressed
 
-    pl.semaphore_wait(barrier, len(greeted))
-
-    def to_owner(k, src, dst, sems):
-        owner = lax.rem(gz + k, WORKERS)
-        pltpu.make_async_remote_copy(
-            src_ref=src.at[owner, :, sems[2]], dst_ref=dst.at[gz, :, sems[2]], send_sem=sems[0], recv_sem=sems[1],
-            device_id=(gx, gy, owner), device_id_type=MESH).start()
-
-    def of_all(ref, sems):
-        return pltpu.make_async_remote_copy(
-            src_ref=ref.at[pl.ds(0, OTHERS), :, sems[2]], dst_ref=ref.at[pl.ds(0, OTHERS), :, sems[2]],
-            send_sem=sems[0], recv_sem=sems[1], device_id=device(partner), device_id_type=MESH)
-
-    var_sems = (var_sem.at[0], var_sem.at[1], slice(None))
-    for k in range(1, WORKERS):
-        to_owner(k, var_sent, var_received, var_sems)
-
-    def exchange_sems(c):
-        return (exchange_send_sem.at[c], exchange_sem.at[c], cols(c))
+    compress(0)
+
+    @pl.loop(1, WORKERS)
+    def _(k):
+        compress(k)
+        to_owner(k, sent, received, exchange_sems(ORDER[0][1]))
 
     def sem_of(nm, c, dr, half=None):
         if nm == "p1":
@@ -240,7 +271,7 @@
         new_master_ref[:, cols(c)] = new_master
 
     updated = []
-    for task in ORDER:
+    for task in ORDER[1:]:
         kind, c = task[0], task[1]
         first, second, third = DIMS[c]
         if kind == "e":
@@ -288,7 +319,7 @@
             src_ref=part, dst_ref=part, send_sem=send_sem, recv_sem=relay_sem,
             device_id=device(partner), device_id_type=MESH).wait_send()
     of_all(var_sent, var_sems).wait_send()
-    for c in range(3):
+    for c in range(COLORS):
         of_all(sent, exchange_sems(c)).wait_send()
 
 
@@ -331,17 +362,17 @@
             pltpu.VMEM((WORKERS, ROWS, PIECE), jnp.bfloat16),
             pltpu.VMEM((ROWS, WIDTH), f32),
             pltpu.SemaphoreType.DMA((3, WORKERS)),
-            pltpu.SemaphoreType.DMA((3,)),
-            pltpu.SemaphoreType.DMA((3,)),
+            pltpu.SemaphoreType.DMA((COLORS,)),
+            pltpu.SemaphoreType.DMA((COLORS,)),
             pltpu.SemaphoreType.DMA((2,)),
-            pltpu.SemaphoreType.DMA((3, 33)),
+            pltpu.SemaphoreType.DMA((COLORS, 33)),
             pltpu.SemaphoreType.DMA,
             pltpu.SemaphoreType.DMA,
             pltpu.SemaphoreType.DMA,
         ],
         compiler_params=pltpu.CompilerParams(collective_id=0, has_side_effects=True, vmem_limit_bytes=36 << 20),
         name="step",
-    )(grads, momentum, variance.T, master)
+    )(*(pltpu.with_memory_space_constraint(a, pltpu.HBM) for a in (grads, momentum, variance.T, master)))
     w = w.reshape(BLOCKS * ROWS, WIDTH)
     weights, new_master, new_momentum, error = pl.pallas_call(
         put_out,

time: 62.2 us -> 57.3 us (0.921)
  local copies, waits for them, and re-layouts: 3.05 us -> 0 us
  Pallas kernels: 58.3 us -> 56.6 us
    unnamed x6 -> x0, local copies, waits for them, and re-layouts: 3.05 us -> none
    pallas_call x1, Pallas kernels: 52.3 us -> 50.5 us  [shards(): pl.pallas_call(step_kernel, out_shape=(pltpu.VMEM((2, 2, 4, 2, 4, ROWS, W...]
where the time goes in v3:
time: 57.3 us; the launch traced here: 57.2 us
  Pallas kernels  56.6 us (99%)
  between operations  0.64 us (1%)
    pallas_call x1, Pallas kernels, shards(): pl.pallas_call(step_kernel, out_shape=(pltpu.VMEM((2, 2, 4, 2, 4, ROWS, W...  50.5 us
    pallas_call x1, Pallas kernels, shards(): pl.pallas_call(put_out, out_shape=(jax.ShapeDtypeStruct((BLOCKS * ROWS, W...  6.04 us

profile of v3, /device:TPU:1, one launch (start us, length us, event | category | flops | bytes accessed | tf_op | source)
XLA Modules:
  0.0 57.2 jit_solution(15500806910636125579)
XLA Ops:
  0.6 50.5 %step.1 = (bf16[2,2,4,2,4,16,3584]{6,5,4,3,2,1,0:T(8,128)(2,1)S(1)}, f32[16,3584]{1,0:T(8,128)S(1)}, f32[16,3584]{1,0:T(8,128)S(1)}, f32[128,3584]{1,0:T(8,128)S(1)}) custom-call(bf16[1,128,3584]{2,1,0:T(8,128)(2,1)} %g_hbm.1, f32[128,3584]{1,0:T(8,128)} %m_hbm.1, f32[448,128]{1,0:T(8,128)} %bitcast.4, f32[16,3584]{1,0:T(8,128)} %master_hbm.1), custom_call_target="tpu_custom_call" | custom-call | tf_op jit(solution)/shard_map/step/pallas_call | solution.py:344
  51.2 6.0 %put_out.1 = (bf16[2048,3584]{1,0:T(8,128)(2,1)}, f32[16,3584]{1,0:T(8,128)}, f32[16,3584]{1,0:T(8,128)}, f32[128,3584]{1,0:T(8,128)}) custom-call(bf16[2048,3584]{1,0:T(8,128)(2,1)S(1)} %bitcast.3, f32[16,3584]{1,0:T(8,128)S(1)} %get-tuple-element.13.new_master, f32[16,3584]{1,0:T(8,128)S(1)} %get-tuple-element.14.new_momentum, ...), custom_call_target="tpu_custom_call" | custom-call | tf_op jit(solution)/shard_map/put_out/pallas_call | solution.py:377
